TPU v7x, 512 devices: a 8x2x16 block of a 8x8x16 slice. The times are simulated.
512 devices in a mesh: groups: 2 (over y), wide: 128 (over x, z), narrow: 2 (over core).
Axes of the slice: x: 8, y: 2, z: 16, core: 2. Of those that a mesh axis runs over, the one named last changes fastest.
The devices are a block of a 8x8x16 slice.
Arguments:
- hidden_in: bfloat16 [102400, 1024], P(('groups', 'wide')), parts along dimension 0, may hold values from -6 to 6
- ffn_gain: bfloat16 [1024], replicated, may hold values from 0.5 to 1.5
- wi_gate: bfloat16 [1024, 2816], P('wide', 'narrow'), may hold values from -0.1875 to 0.1875
- wi_up: bfloat16 [1024, 2816], P('wide', 'narrow'), may hold values from -0.1875 to 0.1875
- wo_down: bfloat16 [2816, 1024], P('narrow', 'wide'), may hold values from -0.109375 to 0.109375
- final_gain: bfloat16 [1024], replicated, may hold values from 0.5 to 1.5
- key_w: bfloat16 [1024, 1024], P('wide', 'narrow'), may hold values from -0.1875 to 0.1875
- value_w: bfloat16 [1024, 1024], P('wide', 'narrow'), may hold values from -0.1875 to 0.1875
- query_w: bfloat16 [1024, 1024], P('wide', 'narrow'), may hold values from -8 to 8
- out_w: bfloat16 [1024, 1024], P('narrow', 'wide'), may hold values from -0.1875 to 0.1875
- dec_gain: bfloat16 [1024], replicated, may hold values from 0.5 to 1.5
- embed: bfloat16 [32128, 1024], P('wide'), may hold values from -6 to 6
- lengths: int32 [512], P(('groups', 'wide')), parts along dimension 0, may hold values from 40 to 200
- answer_ids: int32 [8, 32], P('groups'), parts along dimension 0, may hold values from 0 to 32127
Outputs:
- memory: bfloat16 [102400, 1024], P(('groups', 'wide')), parts along dimension 0
- decoded: bfloat16 [256, 1024], P('groups', 'narrow'), parts along dimension 0
There are 2 independent parts, one for each index of `groups`. A program takes and returns all parts, laid end to end along the dimension named above; an argument that names none is the same for every part. Nothing has to cross between parts.
All inputs are finite; a program needn't handle non-finite values.
Results may differ from a plain program's by a relative error of at most 0.0095.
The roundings to bfloat16 on the way count: a program that leaves them out, or rounds other values in their place, can miss the bound.
Values may be sent and summed in bfloat16 or wider, within the bound.
A program may use at most 64 MiB of HBM per device.

v0:
```python
import math
import jax
import jax.numpy as jnp
from jax import lax
from jax.sharding import Mesh
from jax.sharding import PartitionSpec as P

HEAD_DIM = 64
QUEST = 4
WIDE = ("wide_0", "wide_1")
GROUPS_WIDE = ("groups", "wide_0", "wide_1")
EPS = 1e-06
FLOOR = -1e30


def in_one_piece(arrays, axis, dim, along):
    ends, at = ([], 0)
    for a in arrays[:-1]:
        at += a.shape[along]
        ends.append(at)
    both = jnp.concatenate(arrays, axis=along)
    return tuple(jnp.split(lax.all_gather(both, axis, axis=dim, tiled=True), ends, axis=along))


def in_order(tiles, dim):
    tiles = jnp.moveaxis(tiles, 0, dim)
    lengths = tiles.shape
    return tiles.reshape(*lengths[:dim], lengths[dim] * lengths[dim + 1], *lengths[dim + 2 :])


def all_blocks(x, axes, turns):
    tiles = x
    for k in turns:
        tiles = lax.all_gather(tiles, axes[k])
    done = turns[::-1]
    back = [done.index(k) for k in range(len(axes))]
    tiles = tiles.transpose(*back, *range(len(axes), tiles.ndim))
    return tiles.reshape(-1, *x.shape)


def whole_of(x, axes, turns, dim):
    return in_order(all_blocks(x, axes, turns), dim)


def from_everyone(x, axis):
    copies = jnp.broadcast_to(x, (lax.axis_size(axis), *x.shape))
    return lax.all_to_all(copies, axis, split_axis=0, concat_axis=0, tiled=True)


def over_copies(x, axis):
    return from_everyone(x, axis).sum(axis=0)


def collected_together(x, axis):
    leaves = jax.tree.leaves(x)
    turns = sorted(range(len(leaves)), key=lambda k: -leaves[k].size)
    width = (1, *leaves[turns[0]].shape)[-1]
    lines = [
        jnp.pad(leaves[k].reshape(-1), (0, -leaves[k].size % width)).reshape(-1, width)
        for k in turns
    ]
    both, at, found = (lax.all_gather(jnp.concatenate(lines), axis), 0, {})
    for k, line in zip(turns, lines):
        piece = both[:, at : at + len(line)].reshape(len(both), -1)
        found[k] = piece[:, : leaves[k].size].reshape(-1, *leaves[k].shape)
        at += len(line)
    numbers = iter(range(len(leaves)))
    return jax.tree.map(lambda _: found[next(numbers)], x)


def joined_all(x, axes, combine):
    for axis in axes:
        pieces = collected_together(x, axis)
        x = jax.tree.map(lambda part: part[0], pieces)
        for k in range(1, lax.axis_size(axis)):
            x = combine(x, jax.tree.map(lambda part: part[k], pieces))
    return x


def split_up(x, dim, devices):
    lengths = x.shape
    tiles = x.reshape(*lengths[:dim], devices, lengths[dim] // devices, *lengths[dim + 1 :])
    return jnp.moveaxis(tiles, dim, 0)


def sum_at_owner(x, axis, dim):
    tiles = split_up(x, dim, lax.axis_size(axis))
    arrived = lax.all_to_all(tiles, axis, split_axis=0, concat_axis=0, tiled=True)
    return arrived.astype(jnp.float32).sum(axis=0)


def rms_scale(values, gain):
    mean_square = jnp.mean(values * values, axis=-1, keepdims=True)
    return values * lax.rsqrt(mean_square + EPS) * gain.astype(jnp.float32)


def join_partial(first, second):
    top_first, total_first, acc_first = first
    top_second, total_second, acc_second = second
    top = jnp.maximum(top_first, top_second)
    factor_first = jnp.exp(top_first - top)
    factor_second = jnp.exp(top_second - top)
    width = acc_first.shape[1] // top.shape[1]
    total = total_first * factor_first + total_second * factor_second
    acc = acc_first * jnp.repeat(factor_first, width, axis=1) + acc_second * jnp.repeat(
        factor_second, width, axis=1
    )
    return (top, total, acc)


def per_device(
    hidden_in,
    ffn_gain,
    wi_gate,
    wi_up,
    wo_down,
    final_gain,
    key_w,
    value_w,
    query_w,
    out_w,
    dec_gain,
    embed,
    lengths,
    answer_ids,
):
    rows = hidden_in.shape[0]
    resid_in = hidden_in.astype(jnp.float32)
    enc_in = rms_scale(resid_in, ffn_gain).astype(jnp.bfloat16)
    gate_full, up_full = in_one_piece((wi_gate, wi_up), WIDE, 0, 1)
    gate = jnp.dot(enc_in, gate_full, preferred_element_type=jnp.float32)
    up = jnp.dot(enc_in, up_full, preferred_element_type=jnp.float32)
    inner = (jax.nn.gelu(gate, approximate=True) * up).astype(jnp.bfloat16)
    down_full = whole_of(wo_down, WIDE, (0, 1), 1)
    partial_down = jnp.dot(inner, down_full, preferred_element_type=jnp.float32)
    resid = resid_in + over_copies(partial_down, "narrow")
    memory = rms_scale(resid, final_gain).astype(jnp.bfloat16)
    pass_dev = lengths.shape[0]
    per_question = pass_dev * lax.axis_size(WIDE) // QUEST
    question = lax.axis_index(WIDE) * pass_dev // per_question
    answers = answer_ids.shape[1]
    qrows = answer_ids.shape[0] * answers
    vocab_rows = embed.shape[0]
    local_ids = answer_ids.reshape(qrows) - lax.axis_index(WIDE) * vocab_rows
    onehot = (local_ids[:, None] == jnp.arange(vocab_rows, dtype=jnp.int32)[None, :]).astype(
        jnp.bfloat16
    )
    embedded = lax.psum(jnp.dot(onehot, embed, preferred_element_type=jnp.float32), WIDE)
    dec_in = rms_scale(embedded, dec_gain).astype(jnp.bfloat16)
    own_rows = lax.dynamic_slice_in_dim(dec_in, question * answers, answers, 0)
    proj_cols = key_w.shape[1]
    key_full, value_full, query_full = in_one_piece((key_w, value_w, query_w), WIDE, 0, 1)
    keys_sum = jnp.dot(memory, key_full, preferred_element_type=jnp.float32)
    values_sum = jnp.dot(memory, value_full, preferred_element_type=jnp.float32)
    query_sum = jnp.dot(own_rows, query_full, preferred_element_type=jnp.float32)
    keys = keys_sum.astype(jnp.bfloat16)
    values = values_sum.astype(jnp.bfloat16)
    query = query_sum.astype(jnp.bfloat16)
    heads_local = proj_cols // HEAD_DIM
    query_three = query.reshape(answers, heads_local, HEAD_DIM)
    keys_three = keys.reshape(rows, heads_local, HEAD_DIM)
    values_three = values.reshape(rows, heads_local, HEAD_DIM).astype(jnp.float32)
    scores = jnp.einsum(
        "ahd,khd->ahk", query_three, keys_three, preferred_element_type=jnp.float32
    ) * (1.0 / math.sqrt(HEAD_DIM))
    passage_len = rows // pass_dev
    live = (jnp.arange(passage_len, dtype=jnp.int32)[None, :] < lengths[:, None]).reshape(rows)
    scores = jnp.where(live[None, None, :], scores, FLOOR)
    top = jnp.max(scores, axis=2)
    weights = jnp.exp(scores - top[:, :, None])
    total = jnp.sum(weights, axis=2)
    acc = jnp.einsum("ahk,khd->ahd", weights, values_three).reshape(answers, proj_cols)
    start_row = question * answers
    top_all = lax.dynamic_update_slice_in_dim(
        jnp.full((qrows, heads_local), FLOOR, jnp.float32), top, start_row, 0
    )
    total_all = lax.dynamic_update_slice_in_dim(
        jnp.zeros((qrows, heads_local), jnp.float32), total, start_row, 0
    )
    acc_all = lax.dynamic_update_slice_in_dim(
        jnp.zeros((qrows, proj_cols), jnp.float32), acc, start_row, 0
    )
    top_all, total_all, acc_all = joined_all((top_all, total_all, acc_all), WIDE, join_partial)
    attended = (acc_all / jnp.repeat(total_all, HEAD_DIM, axis=1)).astype(jnp.bfloat16)
    out_full = whole_of(out_w, WIDE, (0, 1), 1)
    partial_out = jnp.dot(attended, out_full, preferred_element_type=jnp.float32)
    share_out = sum_at_owner(partial_out.astype(jnp.bfloat16), "narrow", 1)
    out_half = share_out.shape[1]
    embedded_half = lax.dynamic_slice_in_dim(
        embedded, lax.axis_index("narrow") * out_half, out_half, 1
    )
    decoded = (embedded_half + share_out).astype(jnp.bfloat16)
    return (memory, decoded)


def solution(mesh):
    torus = Mesh(
        mesh.devices.reshape(mesh.shape["groups"], 8, 16, mesh.shape["narrow"]),
        ("groups", "wide_0", "wide_1", "narrow"),
    )
    return jax.shard_map(
        per_device,
        mesh=torus,
        in_specs=(
            P(GROUPS_WIDE, None),
            P(),
            P(WIDE, "narrow"),
            P(WIDE, "narrow"),
            P("narrow", WIDE),
            P(),
            P(WIDE, "narrow"),
            P(WIDE, "narrow"),
            P(WIDE, "narrow"),
            P("narrow", WIDE),
            P(),
            P(WIDE, None),
            P(GROUPS_WIDE),
            P("groups", None),
        ),
        out_specs=(P(GROUPS_WIDE, None), P("groups", "narrow")),
        check_vma=False,
    )
```

profile of v0, /device:TPU:65, one launch (start us, length us, event | category | flops | bytes accessed | tf_op | source)
XLA Modules:
  0.0 730.1 jit_solution(12528337579370721748)
XLA Ops:
  10.3 23.2 %all-gather = bf16[11264,8]{0,1:T(8,128)(2,1)} all-gather(bf16[1408,8]{0,1:T(8,128)(2,1)} %param.18), channel_id=2, replica_groups=mesh['groups'=2,'wide_0'=8,'wide_1'=16,'narrow'=2] {'wide_0'}, dimensions={0}, use_global_device_ids=true | all-gather | bytes 202752 | tf_op jit(solution)/shard_map/all_gather | solution.py:34
  38.4 277.3 %all-reduce.2.cloned.1.call-done = f32[128,1024]{1,0:T(8,128)} async-done(((f32[128,1024]{1,0:T(8,128)}), f32[128,1024]{1,0:T(8,128)}) %all-reduce.2.cloned.1.call-update) | async-done | bytes 524304 | tf_op jit(solution)/shard_map/psum | solution.py:148
  317.0 3.8 copy.413
  323.1 111.4 %all-gather.15.cloned.1.call-done = bf16[1024,2816]{1,0:T(8,128)(2,1)} async-done(((bf16[8,2816]{1,0:T(8,128)(2,1)}), bf16[1024,2816]{1,0:T(8,128)(2,1)}) %all-gather.15.cloned.1.call-update) | async-done | bytes 5767184 | tf_op jit(solution)/shard_map/all_gather | solution.py:22
  434.4 4.9 fusion.12
  439.4 6.1 fusion.24
  445.9 15.5 %all_to_all.10 = f32[2,400,1024]{2,1,0:T(8,128)} all-to-all(f32[2,400,1024]{2,1,0:T(8,128)S(1)} %broadcast_in_dim.170), channel_id=1, replica_groups=mesh['groups'=2,'wide_0'=8,'wide_1'=16,'narrow'=2] {'narrow'}, dimensions={0} | all-to-all | bytes 6553600 | tf_op jit(solution)/shard_map/all_to_all | solution.py:47
  461.4 2.4 reduce_sum.55
  465.3 1.8 convolution_convert_fusion
  468.3 1.8 convolution_convert_fusion.1
  471.7 21.1 %all-gather.4 = bf16[4096,8]{0,1:T(8,128)(2,1)} all-gather(bf16[512,8]{0,1:T(8,128)(2,1)S(1)} %copy-done.8), channel_id=6, replica_groups=mesh['groups'=2,'wide_0'=8,'wide_1'=16,'narrow'=2] {'wide_0'}, dimensions={0}, use_global_device_ids=true | all-gather | bytes 73728 | tf_op jit(solution)/shard_map/all_gather | solution.py:34
  493.2 16.7 %all-gather.23.cloned.1.call-done = f32[8,132,512]{2,1,0:T(8,128)} async-done(((f32[1,132,512]{2,1,0:T(8,128)}), f32[8,132,512]{2,1,0:T(8,128)}) %all-gather.23.cloned.1.call-update) | async-done | bytes 2162704 | tf_op jit(solution)/shard_map/all_gather | solution.py:62
  511.2 2.6 fusion.96
  515.5 1.8 copy.514
  522.7 54.6 %all-gather.21.cloned.1.call-done = bf16[128,512,8]{1,2,0:T(8,128)(2,1)} async-done(((bf16[8,512,8]{1,2,0:T(8,128)(2,1)}), bf16[128,512,8]{1,2,0:T(8,128)(2,1)}) %all-gather.21.cloned.1.call-update) | async-done | bytes 1048592 | tf_op jit(solution)/shard_map/all_gather | solution.py:34
  578.6 79.3 %all-gather.25.cloned.1.call-done = f32[16,132,512]{2,1,0:T(8,128)} async-done(((f32[1,132,512]{2,1,0:T(8,128)}), f32[16,132,512]{2,1,0:T(8,128)}) %all-gather.25.cloned.1.call-update) | async-done | bytes 4325392 | tf_op jit(solution)/shard_map/all_gather | solution.py:62
  657.8 3.8 fusion.94
  663.3 1.8 copy.531
  665.1 1.8 copy.530
  668.7 1.8 copy.528
  675.8 1.8 copy.524
  679.4 1.8 copy.522
  706.2 2.6 divide_convert_fusion
  709.3 12.7 %all_to_all.11 = bf16[2,128,512]{2,1,0:T(8,128)(2,1)S(1)} all-to-all(bf16[2,128,512]{2,1,0:T(8,128)(2,1)S(1)} %bitcast.360), channel_id=1, replica_groups=mesh['groups'=2,'wide_0'=8,'wide_1'=16,'narrow'=2] {'narrow'}, dimensions={0} | all-to-all | bytes 524288 | tf_op jit(solution)/shard_map/all_to_all | solution.py:88
  (194 shorter events, 61.5 us)
Async XLA Ops:
  8.0 1.0 copy-start
  8.1 30.0 %copy-start.9 = (bf16[1024]{0:T(1024)(128)(2,1)S(1)}, bf16[1024]{0:T(1024)(128)(2,1)}, u32[]{:S(2)}) copy-start(bf16[1024]{0:T(1024)(128)(2,1)} %param.24) | copy-start | bytes 6148
  8.1 30.0 %copy-start.10 = (s32[2]{0:T(128)S(1)}, s32[2]{0:T(128)}, u32[]{:S(2)}) copy-start(s32[2]{0:T(128)} %param.26) | copy-start | bytes 28
  8.1 30.1 %copy-start.1 = (bf16[400,1024]{1,0:T(8,128)(2,1)S(1)}, bf16[400,1024]{1,0:T(8,128)(2,1)}, u32[]{:S(2)}) copy-start(bf16[400,1024]{1,0:T(8,128)(2,1)} %param.14) | copy-start | bytes 2457604
  8.1 307.7 %all-reduce.2.cloned.1.call-start = ((), (), s32[]{:S(2)}) async-start(), calls=%async_computation.3 | async-start | bytes 1048576 | tf_op jit(solution)/shard_map/psum | solution.py:148
  10.2 306.8 %all-gather.19.cloned.1.call-start = ((), (), s32[]{:S(2)}) async-start(), calls=%async_computation.5 | async-start | bytes 3063808 | tf_op jit(solution)/shard_map/all_gather | solution.py:34
  33.6 287.2 %all-gather.17.cloned.1.call-start = ((), (), s32[]{:S(2)}) async-start(), calls=%async_computation.4 | async-start | bytes 3170304 | tf_op jit(solution)/shard_map/all_gather | solution.py:22
  35.0 399.4 %all-gather.15.cloned.1.call-start = ((), (), s32[]{:S(2)}) async-start(), calls=%async_computation.2 | async-start | bytes 5812224 | tf_op jit(solution)/shard_map/all_gather | solution.py:22
  36.6 473.3 %all-gather.23.cloned.1.call-start = ((), (), s32[]{:S(2)}) async-start(), calls=%async_computation.7 | async-start | bytes 2506752 | tf_op jit(solution)/shard_map/all_gather | solution.py:62
  317.0 3.8 copy-start.2
  464.4 0.9 copy-start.3
  465.2 2.1 copy-start.5
  467.1 1.1 copy-start.4
  470.1 1.6 copy-start.8
  471.6 105.6 %all-gather.21.cloned.1.call-start = ((), (), s32[]{:S(2)}) async-start(), calls=%async_computation.6 | async-start | bytes 1114112 | tf_op jit(solution)/shard_map/all_gather | solution.py:34
  492.9 164.9 %all-gather.25.cloned.1.call-start = ((), (), s32[]{:S(2)}) async-start(), calls=%async_computation.8 | async-start | bytes 4734976 | tf_op jit(solution)/shard_map/all_gather | solution.py:62
  691.4 10.7 %copy-start.6 = (f32[1,2,512]{2,1,0:T(2,128)S(1)}, f32[1,2,512]{2,1,0:T(2,128)}, u32[]{:S(2)}) copy-start(f32[1,2,512]{2,1,0:T(2,128)} %get-tuple-element.67) | copy-start | bytes 12292
  692.2 9.8 %copy-start.7 = (f32[1,2,512]{2,1,0:T(2,128)S(1)}, f32[1,2,512]{2,1,0:T(2,128)}, u32[]{:S(2)}) copy-start(f32[1,2,512]{2,1,0:T(2,128)} %get-tuple-element.76) | copy-start | bytes 12292
Sparse Core Ops, SparseCore 0:
  13.0 302.6 all-reduce.1
  471.8 38.0 all-gather.22
  511.9 65.2 all-gather.20
  579.2 78.5 all-gather.24
Sparse Core Ops, SparseCore 1:
  33.7 106.3 all-gather.18
  143.5 142.1 all-gather.16
  288.5 145.9 all-gather.14
where the time goes:
time: 732 us; the launch traced here: 730 us
  waiting for transfers between devices  540 us (74%)
  blocking collectives  72.5 us (10%)
  local copies, waits for them, and re-layouts  65.7 us (9%)
  matrix products  18.4 us (3%)
  other arithmetic  17 us (2%)
  between operations  16.3 us (2%)
    psum x1, waiting for transfers between devices, per_device(): lax.psum(jnp.dot(onehot, embed, preferred_element_type=jnp.float32), WIDE)  277 us
    all_gather x2, waiting for transfers between devices, in_one_piece(): lax.all_gather(both, axis, axis=dim, tiled=True)  111 us
    all_gather x2, waiting for transfers between devices, collected_together(): both, at, found = (lax.all_gather(jnp.concatenate(lines), axis), 0, {})  95.9 us
    all_gather x2, waiting for transfers between devices, all_blocks(): tiles = lax.all_gather(tiles, axes[k])  54.6 us
    all_gather x2, blocking collectives, all_blocks(): tiles = lax.all_gather(tiles, axes[k])  44.4 us
    unnamed x47, local copies, waits for them, and re-layouts  27.5 us
    squeeze x74, local copies, waits for them, and re-layouts, joined_all(): x = combine(x, jax.tree.map(lambda part: part[k], pieces))  18.4 us
    all_to_all x1, blocking collectives, from_everyone(): return lax.all_to_all(copies, axis, split_axis=0, concat_axis=0, tiled=True)  15.5 us
  transfers between devices with their start and end apart: 7, of which 5 were waited for; matrix products, arithmetic and copies ran while one was open for 4% of the time, Pallas kernels for 0%

commit v1 on v0

--- a/solution.py
+++ b/solution.py
@@ -145,7 +145,9 @@
     onehot = (local_ids[:, None] == jnp.arange(vocab_rows, dtype=jnp.int32)[None, :]).astype(
         jnp.bfloat16
     )
-    embedded = lax.psum(jnp.dot(onehot, embed, preferred_element_type=jnp.float32), WIDE)
+    embedded = lax.psum(
+        lax.psum(jnp.dot(onehot, embed, preferred_element_type=jnp.float32), "wide_1"), "wide_0"
+    )
     dec_in = rms_scale(embedded, dec_gain).astype(jnp.bfloat16)
     own_rows = lax.dynamic_slice_in_dim(dec_in, question * answers, answers, 0)
     proj_cols = key_w.shape[1]

time: 732 us -> 932 us (1.27)
  waiting for transfers between devices: 540 us -> 745 us
    all_gather x2, waiting for transfers between devices: 111 us -> 288 us  [in_one_piece(): lax.all_gather(both, axis, axis=dim, tiled=True)]
    all_gather x2, waiting for transfers between devices: 54.6 us -> 127 us  [all_blocks(): tiles = lax.all_gather(tiles, axes[k])]
    psum x1 -> x2, waiting for transfers between devices: 277 us -> 233 us  [the longest x1 168 us: per_device(): lax.psum(jnp.dot(onehot, embed, preferred_element_type=jnp.float32), 'wid...]
    unnamed x47 -> x61, local copies, waits for them, and re-layouts: 27.5 us -> 27.4 us
  transfers between devices with their start and end apart: 7 -> 8, of which waited for: 5 -> 8; matrix products, arithmetic and copies ran while one was open for 4% -> 2% of each run, Pallas kernels for 0% -> 0%
where the time goes in v1:
time: 932 us; the launch traced here: 931 us
  waiting for transfers between devices  745 us (80%)
  blocking collectives  71.8 us (8%)
  local copies, waits for them, and re-layouts  65.5 us (7%)
  matrix products  18.4 us (2%)
  between operations  15.1 us (2%)
  other arithmetic  14.3 us (2%)
    all_gather x2, waiting for transfers between devices, in_one_piece(): lax.all_gather(both, axis, axis=dim, tiled=True)  288 us
    psum x1, waiting for transfers between devices, per_device(): lax.psum(jnp.dot(onehot, embed, preferred_element_type=jnp.float32), 'wid...  168 us
    all_gather x2, waiting for transfers between devices, all_blocks(): tiles = lax.all_gather(tiles, axes[k])  127 us
    all_gather x2, waiting for transfers between devices, collected_together(): both, at, found = (lax.all_gather(jnp.concatenate(lines), axis), 0, {})  95.5 us
    psum x1, waiting for transfers between devices, per_device(): lax.psum(lax.psum(jnp.dot(onehot, embed, preferred_element_type=jnp.float...  65.2 us
    all_gather x2, blocking collectives, all_blocks(): tiles = lax.all_gather(tiles, axes[k])  43.4 us
    unnamed x61, local copies, waits for them, and re-layouts  27.4 us
  transfers between devices with their start and end apart: 8, of which 8 were waited for; matrix products, arithmetic and copies ran while one was open for 2% of the time, Pallas kernels for 0%

profile of v1, /device:TPU:65, one launch (start us, length us, event | category | flops | bytes accessed | tf_op | source)
XLA Modules:
  0.0 930.7 jit_solution(16681242639916269181)
XLA Ops:
  9.5 167.9 %all-reduce.3.cloned.1.call-done = f32[128,1024]{1,0:T(8,128)} async-done(((f32[128,1024]{1,0:T(8,128)}), f32[128,1024]{1,0:T(8,128)}) %all-reduce.3.cloned.1.call-update) | async-done | bytes 524304 | tf_op jit(solution)/shard_map/psum | solution.py:149
  177.6 22.1 %all-gather = bf16[11264,8]{0,1:T(8,128)(2,1)} all-gather(bf16[1408,8]{0,1:T(8,128)(2,1)} %param.18), channel_id=2, replica_groups=mesh['groups'=2,'wide_0'=8,'wide_1'=16,'narrow'=2] {'wide_0'}, dimensions={0}, use_global_device_ids=true | all-gather | bytes 202752 | tf_op jit(solution)/shard_map/all_gather | solution.py:34
  201.9 65.2 %all-reduce.5.cloned.1.call-done = f32[128,1024]{1,0:T(8,128)} async-done(((f32[128,1024]{1,0:T(8,128)}), f32[128,1024]{1,0:T(8,128)}) %all-reduce.5.cloned.1.call-update) | async-done | bytes 524304 | tf_op jit(solution)/shard_map/psum | solution.py:148
  268.4 72.7 %all-gather.19.cloned.1.call-done = bf16[128,1408,8]{1,2,0:T(8,128)(2,1)} async-done(((bf16[8,1408,8]{1,2,0:T(8,128)(2,1)}), bf16[128,1408,8]{1,2,0:T(8,128)(2,1)}) %all-gather.19.cloned.1.call-update) | async-done | bytes 2883600 | tf_op jit(solution)/shard_map/all_gather | solution.py:34
  341.1 3.7 copy.413
  344.8 141.4 %all-gather.17.cloned.1.call-done = bf16[1024,1536]{1,0:T(8,128)(2,1)} async-done(((bf16[8,1536]{1,0:T(8,128)(2,1)}), bf16[1024,1536]{1,0:T(8,128)(2,1)}) %all-gather.17.cloned.1.call-update) | async-done | bytes 3145744 | tf_op jit(solution)/shard_map/all_gather | solution.py:22
  488.5 147.0 %all-gather.15.cloned.1.call-done = bf16[1024,2816]{1,0:T(8,128)(2,1)} async-done(((bf16[8,2816]{1,0:T(8,128)(2,1)}), bf16[1024,2816]{1,0:T(8,128)(2,1)}) %all-gather.15.cloned.1.call-update) | async-done | bytes 5767184 | tf_op jit(solution)/shard_map/all_gather | solution.py:22
  635.5 4.9 fusion.12
  640.4 6.1 fusion.24
  647.0 15.8 %all_to_all.10 = f32[2,400,1024]{2,1,0:T(8,128)} all-to-all(f32[2,400,1024]{2,1,0:T(8,128)S(1)} %broadcast_in_dim.170), channel_id=1, replica_groups=mesh['groups'=2,'wide_0'=8,'wide_1'=16,'narrow'=2] {'narrow'}, dimensions={0} | all-to-all | bytes 6553600 | tf_op jit(solution)/shard_map/all_to_all | solution.py:47
  662.8 2.4 reduce_sum.55
  666.6 1.8 convolution_convert_fusion
  669.7 1.8 convolution_convert_fusion.1
  673.1 21.2 %all-gather.4 = bf16[4096,8]{0,1:T(8,128)(2,1)} all-gather(bf16[512,8]{0,1:T(8,128)(2,1)S(1)} %copy-done.10), channel_id=6, replica_groups=mesh['groups'=2,'wide_0'=8,'wide_1'=16,'narrow'=2] {'wide_0'}, dimensions={0}, use_global_device_ids=true | all-gather | bytes 73728 | tf_op jit(solution)/shard_map/all_gather | solution.py:34
  694.7 16.1 %all-gather.23.cloned.1.call-done = f32[8,132,512]{2,1,0:T(8,128)} async-done(((f32[1,132,512]{2,1,0:T(8,128)}), f32[8,132,512]{2,1,0:T(8,128)}) %all-gather.23.cloned.1.call-update) | async-done | bytes 2162704 | tf_op jit(solution)/shard_map/all_gather | solution.py:62
  712.1 2.6 fusion.96
  723.6 54.7 %all-gather.21.cloned.1.call-done = bf16[128,512,8]{1,2,0:T(8,128)(2,1)} async-done(((bf16[8,512,8]{1,2,0:T(8,128)(2,1)}), bf16[128,512,8]{1,2,0:T(8,128)(2,1)}) %all-gather.21.cloned.1.call-update) | async-done | bytes 1048592 | tf_op jit(solution)/shard_map/all_gather | solution.py:34
  779.6 79.4 %all-gather.25.cloned.1.call-done = f32[16,132,512]{2,1,0:T(8,128)} async-done(((f32[1,132,512]{2,1,0:T(8,128)}), f32[16,132,512]{2,1,0:T(8,128)}) %all-gather.25.cloned.1.call-update) | async-done | bytes 4325392 | tf_op jit(solution)/shard_map/all_gather | solution.py:62
  859.0 3.8 fusion.94
  864.5 1.8 copy.531
  868.0 1.8 copy.529
  871.6 1.8 copy.527
  907.3 2.6 divide_convert_fusion
  910.4 12.7 %all_to_all.11 = bf16[2,128,512]{2,1,0:T(8,128)(2,1)S(1)} all-to-all(bf16[2,128,512]{2,1,0:T(8,128)(2,1)S(1)} %bitcast.360), channel_id=1, replica_groups=mesh['groups'=2,'wide_0'=8,'wide_1'=16,'narrow'=2] {'narrow'}, dimensions={0} | all-to-all | bytes 524288 | tf_op jit(solution)/shard_map/all_to_all | solution.py:88
  (211 shorter events, 64.2 us)
Async XLA Ops:
  7.2 1.2 copy-start
  7.2 192.7 %copy-start.11 = (bf16[8,512]{1,0:T(8,128)(2,1)S(1)}, bf16[8,512]{1,0:T(8,128)(2,1)}, u32[]{:S(2)}) copy-start(bf16[8,512]{1,0:T(8,128)(2,1)} %param.22) | copy-start | bytes 24580
  7.2 192.7 %copy-start.12 = (bf16[8,512]{1,0:T(8,128)(2,1)S(1)}, bf16[8,512]{1,0:T(8,128)(2,1)}, u32[]{:S(2)}) copy-start(bf16[8,512]{1,0:T(8,128)(2,1)} %param.21) | copy-start | bytes 24580
  7.2 192.7 %copy-start.13 = (bf16[8,512]{1,0:T(8,128)(2,1)S(1)}, bf16[8,512]{1,0:T(8,128)(2,1)}, u32[]{:S(2)}) copy-start(bf16[8,512]{1,0:T(8,128)(2,1)} %param.20) | copy-start | bytes 24580
  7.2 193.4 %copy-start.6 = (bf16[8,1408]{1,0:T(8,128)(2,1)S(1)}, bf16[8,1408]{1,0:T(8,128)(2,1)}, u32[]{:S(2)}) copy-start(bf16[8,1408]{1,0:T(8,128)(2,1)} %param.17) | copy-start | bytes 67588
  7.2 193.4 %copy-start.7 = (bf16[8,1408]{1,0:T(8,128)(2,1)S(1)}, bf16[8,1408]{1,0:T(8,128)(2,1)}, u32[]{:S(2)}) copy-start(bf16[8,1408]{1,0:T(8,128)(2,1)} %param.16) | copy-start | bytes 67588
  7.2 194.2 %copy-start.14 = (bf16[1024]{0:T(1024)(128)(2,1)S(1)}, bf16[1024]{0:T(1024)(128)(2,1)}, u32[]{:S(2)}) copy-start(bf16[1024]{0:T(1024)(128)(2,1)} %param.15) | copy-start | bytes 6148
  7.3 194.2 %copy-start.15 = (bf16[1024]{0:T(1024)(128)(2,1)S(1)}, bf16[1024]{0:T(1024)(128)(2,1)}, u32[]{:S(2)}) copy-start(bf16[1024]{0:T(1024)(128)(2,1)} %param.19) | copy-start | bytes 6148
  7.3 194.2 %copy-start.16 = (bf16[1024]{0:T(1024)(128)(2,1)S(1)}, bf16[1024]{0:T(1024)(128)(2,1)}, u32[]{:S(2)}) copy-start(bf16[1024]{0:T(1024)(128)(2,1)} %param.24) | copy-start | bytes 6148
  7.3 194.2 %copy-start.17 = (s32[2]{0:T(128)S(1)}, s32[2]{0:T(128)}, u32[]{:S(2)}) copy-start(s32[2]{0:T(128)} %param.26) | copy-start | bytes 28
  7.3 194.4 %copy-start.1 = (bf16[400,1024]{1,0:T(8,128)(2,1)S(1)}, bf16[400,1024]{1,0:T(8,128)(2,1)}, u32[]{:S(2)}) copy-start(bf16[400,1024]{1,0:T(8,128)(2,1)} %param.14) | copy-start | bytes 2457604
  7.3 170.1 %all-reduce.3.cloned.1.call-start = ((), (), s32[]{:S(2)}) async-start(), calls=%async_computation.3 | async-start | bytes 1048576 | tf_op jit(solution)/shard_map/psum | solution.py:149
  9.5 257.7 %all-reduce.5.cloned.1.call-start = ((), (), s32[]{:S(2)}) async-start(), calls=%async_computation.4 | async-start | bytes 1048576 | tf_op jit(solution)/shard_map/psum | solution.py:148
  177.5 163.6 %all-gather.19.cloned.1.call-start = ((), (), s32[]{:S(2)}) async-start(), calls=%async_computation.6 | async-start | bytes 3063808 | tf_op jit(solution)/shard_map/all_gather | solution.py:34
  199.8 286.4 %all-gather.17.cloned.1.call-start = ((), (), s32[]{:S(2)}) async-start(), calls=%async_computation.5 | async-start | bytes 3170304 | tf_op jit(solution)/shard_map/all_gather | solution.py:22
  200.6 434.9 %all-gather.15.cloned.1.call-start = ((), (), s32[]{:S(2)}) async-start(), calls=%async_computation.2 | async-start | bytes 5812224 | tf_op jit(solution)/shard_map/all_gather | solution.py:22
  201.3 509.5 %all-gather.23.cloned.1.call-start = ((), (), s32[]{:S(2)}) async-start(), calls=%async_computation.8 | async-start | bytes 2506752 | tf_op jit(solution)/shard_map/all_gather | solution.py:62
  341.1 145.1 %copy-start.2 = (f32[128,1024]{1,0:T(8,128)S(1)}, f32[128,1024]{1,0:T(8,128)}, u32[]{:S(2)}) copy-start(f32[128,1024]{1,0:T(8,128)} %all-reduce.5.cloned.1.call-done) | copy-start | bytes 1572868
  666.6 2.1 copy-start.5
  671.5 1.6 copy-start.10
  673.0 105.3 %all-gather.21.cloned.1.call-start = ((), (), s32[]{:S(2)}) async-start(), calls=%async_computation.7 | async-start | bytes 1114112 | tf_op jit(solution)/shard_map/all_gather | solution.py:34
  694.4 164.6 %all-gather.25.cloned.1.call-start = ((), (), s32[]{:S(2)}) async-start(), calls=%async_computation.9 | async-start | bytes 4734976 | tf_op jit(solution)/shard_map/all_gather | solution.py:62
  892.6 10.7 %copy-start.8 = (f32[1,2,512]{2,1,0:T(2,128)S(1)}, f32[1,2,512]{2,1,0:T(2,128)}, u32[]{:S(2)}) copy-start(f32[1,2,512]{2,1,0:T(2,128)} %get-tuple-element.67) | copy-start | bytes 12292
  893.3 9.8 %copy-start.9 = (f32[1,2,512]{2,1,0:T(2,128)S(1)}, f32[1,2,512]{2,1,0:T(2,128)}, u32[]{:S(2)}) copy-start(f32[1,2,512]{2,1,0:T(2,128)} %get-tuple-element.76) | copy-start | bytes 12292
  (2 other events, 2.0 us)
Sparse Core Ops, SparseCore 0:
  11.0 166.3 all-reduce.2
  179.8 87.3 all-reduce.4
  269.3 71.7 all-gather.18
  344.5 141.6 all-gather.16
  489.6 145.8 all-gather.14
  673.2 37.5 all-gather.22
  712.9 65.3 all-gather.20
  780.4 78.5 all-gather.24
